TPU v7x, 32 devices: a whole 2x2x4 slice. The times are simulated.
32 devices in a mesh: row: 4 (over z), col: 8 (over y, x, core).
Axes of the slice: x: 2, y: 2, z: 4, core: 2. Of those that a mesh axis runs over, the one named last changes fastest.
Arguments:
- pencil_a: float32 [4, 3072, 8, 1536], P('row', None, 'col'), may hold values from -6 to 6, as said below
- pencil_b: float32 [4, 3072, 8, 1536], P('row', None, 'col'), may hold values from -6 to 6
Outputs:
- new_a: float32 [4, 3072, 8, 1536], P('row', None, 'col')
- new_b: float32 [4, 3072, 8, 1536], P('row', None, 'col')
Inputs may be any that keep to these rules, and one draw needn't show every extreme that they name: `pencil_a`: the first 256 columns of Amat are zero in the last 256 rows of Amat.
All inputs are finite; a program needn't handle non-finite values.
Results may differ from a plain program's by a relative error of at most 0.000056.
Values sent between devices are 32-bit elements; how exact they have to be, the bound alone decides.
A program may use at most 192 MiB of HBM per device.

v0:
```python
import jax
import jax.numpy as jnp
from jax import lax
from jax.sharding import PartitionSpec as P

NB = 256


def broadcast(array, axis, root):
    mine = lax.axis_index(axis) == root
    return lax.psum(jnp.where(mine, array, jnp.zeros_like(array)), axis)


def matmul(left, right):
    return jnp.dot(left, right, precision=lax.Precision.HIGHEST, preferred_element_type=jnp.float32)


def inverse_factor(gram):
    lower = jnp.linalg.cholesky(gram)
    ident = jnp.eye(gram.shape[0], dtype=jnp.float32)
    return jax.scipy.linalg.solve_triangular(lower, ident, lower=True).T


def general_inverse(square):
    lower = jnp.linalg.cholesky(matmul(square, square.T))
    ident = jnp.eye(square.shape[0], dtype=jnp.float32)
    linv = jax.scipy.linalg.solve_triangular(lower, ident, lower=True)
    return matmul(square.T, matmul(linv.T, linv))


def on_device(pencil_a, pencil_b):
    rows_loc = pencil_a.shape[1]
    cols_loc = pencil_a.shape[3]
    amat = pencil_a.reshape(rows_loc, cols_loc)
    bmat = pencil_b.reshape(rows_loc, cols_loc)
    width = NB
    ident = jnp.eye(width, dtype=jnp.float32)
    last_row = lax.axis_size("row") - 1
    last_col = lax.axis_size("col") - 1
    top_mask = (lax.axis_index("row") == 0).astype(jnp.float32)
    end_mask = (lax.axis_index("col") == last_col).astype(jnp.float32)
    panel = broadcast(amat[:, :width], "col", 0)
    gram_one = lax.psum(matmul(panel.T, panel), "row")
    first_inv = inverse_factor(gram_one)
    basis = matmul(panel, first_inv)
    top_block = broadcast(basis[:width], "row", 0)
    kinv_left = general_inverse(ident + top_block)
    vectors = basis + top_mask * jnp.pad(ident, ((0, rows_loc - width), (0, 0)))
    products_a, products_b = lax.psum((matmul(vectors.T, amat), matmul(vectors.T, bmat)), "row")
    amat = amat - matmul(vectors, matmul(kinv_left, products_a))
    bmat = bmat - matmul(vectors, matmul(kinv_left, products_b))
    strip = broadcast(bmat[rows_loc - width :], "row", last_row)
    gram_one = lax.psum(matmul(strip, strip.T), "col")
    first_inv = inverse_factor(gram_one)
    basis_t = matmul(first_inv.T, strip)
    end_block = broadcast(basis_t[:, cols_loc - width :], "col", last_col)
    kinv_right = general_inverse(ident + end_block.T)
    vectors_t = basis_t + end_mask * jnp.pad(ident, ((0, 0), (cols_loc - width, 0)))
    rows_a = amat
    rows_b = bmat
    share = lax.psum_scatter(
        jnp.concatenate([matmul(rows_a, vectors_t.T), matmul(rows_b, vectors_t.T)], axis=1),
        "col",
        scatter_dimension=0,
        tiled=True,
    )
    scaled = jnp.concatenate(
        [matmul(share[:, :width], kinv_right.T), matmul(share[:, width:], kinv_right.T)], axis=1
    )
    gathered = lax.all_gather(scaled, "col", axis=0, tiled=True)
    mixed_a = gathered[:, :width]
    mixed_b = gathered[:, width:]
    amat = amat - matmul(mixed_a, vectors_t)
    bmat = bmat - matmul(mixed_b, vectors_t)
    return (amat.reshape(1, rows_loc, 1, cols_loc), bmat.reshape(1, rows_loc, 1, cols_loc))


def solution(mesh):
    placed = (P("row", None, "col", None), P("row", None, "col", None))
    return jax.shard_map(
        on_device,
        mesh=mesh,
        in_specs=placed,
        out_specs=(P("row", None, "col", None), P("row", None, "col", None)),
        check_vma=False,
    )
```

profile of v0, /device:TPU:0, one launch (start us, length us, event | category | flops | bytes accessed | tf_op | source)
XLA Modules:
  0.0 944.9 jit_solution(2543293322274837109)
XLA Ops:
  7.2 16.4 %copy.42 = f32[1,3072,1,1536]{3,1,2,0:T(8,128)} copy(f32[1,3072,1,1536]{3,2,1,0:T(1,128)} %param.5) | data formatting | bytes 37748736
  23.6 3.8 slice_select_fusion
  27.5 72.1 %all-reduce.12.cloned.1.call-done = f32[3072,256]{1,0:T(8,128)} async-done(((f32[3072,256]{1,0:T(8,128)}), f32[3072,256]{1,0:T(8,128)}) %all-reduce.12.cloned.1.call-update) | async-done | bytes 3145744 | tf_op jit(solution)/shard_map/psum | solution.py:11
  99.6 8.6 fusion.87
  108.5 35.5 %all-reduce.14.cloned.1.call-done = f32[256,256]{0,1:T(8,128)} async-done(((f32[256,256]{0,1:T(8,128)}), f32[256,256]{0,1:T(8,128)}) %all-reduce.14.cloned.1.call-update) | async-done | bytes 262160 | tf_op jit(solution)/shard_map/psum | solution.py:43
  146.1 11.7 %cholesky.214 = f32[128,128]{1,0:T(8,128)S(1)} custom-call(f32[128,128]{1,0:T(8,128)S(1)} %cholesky.346), custom_call_target="Cholesky" | custom-call | tf_op jit(solution)/shard_map/jit(cholesky)/cholesky | solution.py:19
  157.9 9.8 %custom-call.17 = f32[1,128,128]{1,2,0:T(8,128)S(1)} custom-call(f32[1,128,128]{2,1,0:T(8,128)S(1)} %get-tuple-element.95), custom_call_target="InvertDiagBlocksLowerTriangular" | custom-call | tf_op jit(solution)/shard_map/jit(cholesky)/cholesky | solution.py:19
  168.2 11.7 %cholesky.231 = f32[128,128]{1,0:T(8,128)S(1)} custom-call(f32[128,128]{1,0:T(8,128)S(1)} %convolution_subtract_fusion.8), custom_call_target="Cholesky" | custom-call | tf_op jit(solution)/shard_map/jit(cholesky)/cholesky | solution.py:19
  181.9 4.2 while.8
  186.1 19.7 %custom-call.18 = f32[2,128,128]{1,2,0:T(8,128)S(1)} custom-call(f32[2,128,128]{2,1,0:T(8,128)S(1)} %get-tuple-element.30), custom_call_target="InvertDiagBlocksLowerTriangular" | custom-call | tf_op jit(solution)/shard_map/jit(_solve_triangular)/triangular_solve | solution.py:21
  206.7 4.5 fusion.12
  212.0 22.7 %fusion = f32[256,1536]{1,0:T(8,128)} fusion(f32[1,3072,1,1536]{3,2,1,0:T(1,128)} %param.6, f32[3072,256]{1,0:T(8,128)S(1)} %fusion.12, f32[256,256]{1,0:T(8,128)S(1)} %fusion.32, f32[]{:T(128)S(6)} %convert_element_type.32), kind=kOutput, calls=%fused_computation.9 | convolution fusion | flops 14497087488 | bytes 23855108 | tf_op jit(solution)/shard_map/dot_general | solution.py:15
  234.8 22.6 %fusion.5 = f32[256,1536]{1,0:T(8,128)} fusion(f32[3072,256]{1,0:T(8,128)S(1)} %fusion.12, f32[256,256]{1,0:T(8,128)S(1)} %fusion.32, f32[]{:T(128)S(6)} %convert_element_type.32, f32[1,3072,1,1536]{3,2,1,0:T(1,128)} %param.5), kind=kOutput, calls=%fused_computation.31 | convolution fusion | flops 14497087488 | bytes 23855108 | tf_op jit(solution)/shard_map/dot_general | solution.py:15
  257.4 55.0 %all-reduce.22.cloned.1.call-done = (f32[256,256]{1,0:T(8,128)}, f32[256,1536]{1,0:T(8,128)}) async-done(((f32[256,256]{1,0:T(8,128)}, f32[256,1536]{1,0:T(8,128)}), (f32[256,256]{1,0:T(8,128)}, f32[256,1536]{1,0:T(8,128)})) %all-reduce.22.cloned.1.call-update) | async-done | bytes 1835024 | tf_op jit(solution)/shard_map/psum | solution.py:11
  312.4 2.1 fusion.37
  318.1 11.7 %cholesky.248 = f32[128,128]{1,0:T(8,128)S(1)} custom-call(f32[128,128]{1,0:T(8,128)S(1)} %cholesky.349), custom_call_target="Cholesky" | custom-call | tf_op jit(solution)/shard_map/jit(cholesky)/cholesky | solution.py:25
  330.5 10.4 %custom-call.19 = f32[1,128,128]{1,2,0:T(8,128)} custom-call(f32[1,128,128]{2,1,0:T(8,128)S(1)} %get-tuple-element.91), custom_call_target="InvertDiagBlocksLowerTriangular" | custom-call | tf_op jit(solution)/shard_map/jit(cholesky)/cholesky | solution.py:25
  344.5 11.7 %cholesky.265 = f32[128,128]{1,0:T(8,128)S(1)} custom-call(f32[128,128]{1,0:T(8,128)S(1)} %convolution_subtract_fusion.7), custom_call_target="Cholesky" | custom-call | tf_op jit(solution)/shard_map/jit(cholesky)/cholesky | solution.py:25
  360.4 5.7 while.9
  361.0 2.3 bitcast_dynamic-update-slice_fusion.9
  363.9 2.2 bitcast_dynamic-update-slice_fusion.9
  366.7 20.9 %custom-call.20 = f32[2,128,128]{1,2,0:T(8,128)S(1)} custom-call(f32[2,128,128]{2,1,0:T(8,128)} %copy-done.7), custom_call_target="InvertDiagBlocksLowerTriangular" | custom-call | tf_op jit(solution)/shard_map/jit(_solve_triangular)/triangular_solve | solution.py:27
  393.8 22.1 %bitcast_subtract_fusion = f32[3072,1536]{1,0:T(8,128)S(1)} fusion(f32[1,3072,1,1536]{3,2,1,0:T(1,128)} %param.6, f32[256,1536]{1,0:T(8,128)S(1)} %fusion.89, f32[3072,256]{1,0:T(8,128)S(1)} %fusion.12, f32[256,256]{1,0:T(8,128)S(1)} %fusion.32, f32[]{:T(128)S(6)} %convert_element_type.32), kind=kOutput, calls=%fused_computation.8 | convolution fusion | flops 14501806080 | bytes 42729476 | tf_op jit(solution)/shard_map/dot_general | solution.py:15
  415.9 6.5 copy-done
  423.9 120.0 %all-reduce.20.cloned.1.call-done = (f32[256,1536]{1,0:T(8,128)}, f32[256,1536]{1,0:T(8,128)}) async-done(((f32[256,1536]{1,0:T(8,128)}, f32[256,1536]{1,0:T(8,128)}), (f32[256,1536]{1,0:T(8,128)}, f32[256,1536]{1,0:T(8,128)})) %all-reduce.20.cloned.1.call-update) | async-done | bytes 3145744 | tf_op jit(solution)/shard_map/psum | solution.py:49
  543.9 4.2 fusion.88
  548.1 2.2 fusion.90
  550.3 23.5 %convolution_subtract_fusion = f32[3072,1536]{1,0:T(8,128)} fusion(f32[256,1536]{1,0:T(8,128)} %fusion.88, f32[3072,256]{1,0:T(8,128)S(1)} %fusion.12, f32[256,256]{1,0:T(8,128)S(1)} %fusion.32, f32[]{:T(128)S(6)} %convert_element_type.32, f32[1,3072,1,1536]{3,2,1,0:T(1,128)} %param.5), kind=kOutput, calls=%fused_computation.15 | convolution fusion | flops 14501806080 | bytes 42729476 | tf_op jit(solution)/shard_map/dot_general | solution.py:15
  573.9 29.5 %all-reduce.16.cloned.1.call-done = f32[256,256]{0,1:T(8,128)} async-done(((f32[256,256]{0,1:T(8,128)}), f32[256,256]{0,1:T(8,128)}) %all-reduce.16.cloned.1.call-update) | async-done | bytes 262160 | tf_op jit(solution)/shard_map/psum | solution.py:53
  605.4 11.7 %cholesky.282 = f32[128,128]{1,0:T(8,128)S(1)} custom-call(f32[128,128]{1,0:T(8,128)S(1)} %cholesky.352), custom_call_target="Cholesky" | custom-call | tf_op jit(solution)/shard_map/jit(cholesky)/cholesky | solution.py:19
  617.8 9.8 %custom-call.21 = f32[1,128,128]{1,2,0:T(8,128)S(1)} custom-call(f32[1,128,128]{2,1,0:T(8,128)S(1)} %get-tuple-element.87), custom_call_target="InvertDiagBlocksLowerTriangular" | custom-call | tf_op jit(solution)/shard_map/jit(cholesky)/cholesky | solution.py:19
  628.1 11.7 %cholesky.299 = f32[128,128]{1,0:T(8,128)S(1)} custom-call(f32[128,128]{1,0:T(8,128)S(1)} %convolution_subtract_fusion.6), custom_call_target="Cholesky" | custom-call | tf_op jit(solution)/shard_map/jit(cholesky)/cholesky | solution.py:19
  642.0 4.1 while.10
  646.1 19.7 %custom-call.22 = f32[2,128,128]{1,2,0:T(8,128)S(1)} custom-call(f32[2,128,128]{2,1,0:T(8,128)S(1)} %get-tuple-element.32), custom_call_target="InvertDiagBlocksLowerTriangular" | custom-call | tf_op jit(solution)/shard_map/jit(_solve_triangular)/triangular_solve | solution.py:21
  669.2 20.7 %fusion.10 = f32[3072,256]{0,1:T(8,128)S(1)} fusion(f32[3072,1536]{1,0:T(8,128)} %copy-done, f32[256,1536]{1,0:T(8,128)S(1)} %fusion.20, f32[256,256]{1,0:T(8,128)S(1)} %fusion.32, f32[]{:T(128)S(6)} %convert_element_type.33), kind=kOutput, calls=%fused_computation.37 | convolution fusion | flops 14496301056 | bytes 23855108 | tf_op jit(solution)/shard_map/dot_general | solution.py:15
  689.9 20.3 %fusion.11 = f32[3072,256]{0,1:T(8,128)S(1)} fusion(f32[3072,1536]{1,0:T(8,128)} %convolution_subtract_fusion, f32[256,1536]{1,0:T(8,128)S(1)} %fusion.20, f32[256,256]{1,0:T(8,128)S(1)} %fusion.32, f32[]{:T(128)S(6)} %convert_element_type.33), kind=kOutput, calls=%fused_computation.38 | convolution fusion | flops 14496301056 | bytes 23855108 | tf_op jit(solution)/shard_map/dot_general | solution.py:15
  710.2 3.1 pad_maximum_fusion
  713.5 9.0 all-reduce.18.cloned.1.call-done
  724.3 11.7 %cholesky.316 = f32[128,128]{1,0:T(8,128)S(1)} custom-call(f32[128,128]{1,0:T(8,128)S(1)} %cholesky.355), custom_call_target="Cholesky" | custom-call | tf_op jit(solution)/shard_map/jit(cholesky)/cholesky | solution.py:25
  736.0 9.8 %custom-call.23 = f32[1,128,128]{1,2,0:T(8,128)S(1)} custom-call(f32[1,128,128]{2,1,0:T(8,128)S(1)} %get-tuple-element.83), custom_call_target="InvertDiagBlocksLowerTriangular" | custom-call | tf_op jit(solution)/shard_map/jit(cholesky)/cholesky | solution.py:25
  746.4 11.7 %cholesky.333 = f32[128,128]{1,0:T(8,128)S(1)} custom-call(f32[128,128]{1,0:T(8,128)S(1)} %convolution_subtract_fusion.5), custom_call_target="Cholesky" | custom-call | tf_op jit(solution)/shard_map/jit(cholesky)/cholesky | solution.py:25
  760.6 4.0 while.11
  764.6 19.7 %custom-call.24 = f32[2,128,128]{1,2,0:T(8,128)S(1)} custom-call(f32[2,128,128]{2,1,0:T(8,128)S(1)} %get-tuple-element.33), custom_call_target="InvertDiagBlocksLowerTriangular" | custom-call | tf_op jit(solution)/shard_map/jit(_solve_triangular)/triangular_solve | solution.py:27
  791.9 45.4 %all-gather.2.cloned.1.call-done = f32[3072,512]{0,1:T(8,128)} async-done(((f32[384,512]{0,1:T(8,128)}), f32[3072,512]{0,1:T(8,128)}) %all-gather.2.cloned.1.call-update) | async-done | bytes 6291472 | tf_op jit(solution)/shard_map/all_gather | solution.py:70
  837.3 35.2 %subtract_bitcast_fusion.1 = f32[1,3072,1,1536]{3,1,2,0:T(8,128)} fusion(f32[3072,1536]{1,0:T(8,128)} %convolution_subtract_fusion, f32[3072,512]{0,1:T(8,128)} %all-gather.2.cloned.1.call-done, f32[256,1536]{1,0:T(8,128)S(1)} %fusion.20, f32[256,256]{1,0:T(8,128)S(1)} %fusion.32, f32[]{:T(128)S(6)} %convert_element_type.33), kind=kOutput, calls=%fused_computation.13 | convolution fusion | flops 14501019648 | bytes 42729476 | tf_op jit(solution)/shard_map/dot_general | solution.py:15
  872.5 22.5 %copy.12 = f32[1,3072,1,1536]{3,2,1,0:T(1,128)} copy(f32[1,3072,1,1536]{3,1,2,0:T(8,128)} %subtract_bitcast_fusion.1) | data formatting | bytes 37748736
  895.1 20.5 %subtract_bitcast_fusion = f32[1,3072,1,1536]{3,1,2,0:T(8,128)} fusion(f32[3072,1536]{1,0:T(8,128)S(1)} %bitcast.159, f32[3072,512]{0,1:T(8,128)} %all-gather.2.cloned.1.call-done, f32[256,1536]{1,0:T(8,128)S(1)} %fusion.20, f32[256,256]{1,0:T(8,128)S(1)} %fusion.32, f32[]{:T(128)S(6)} %convert_element_type.33), kind=kOutput, calls=%fused_computation.12 | convolution fusion | flops 14501019648 | bytes 42729476 | tf_op jit(solution)/shard_map/dot_general | solution.py:15
  915.6 22.3 %copy.13 = f32[1,3072,1,1536]{3,2,1,0:T(1,128)} copy(f32[1,3072,1,1536]{3,1,2,0:T(8,128)} %subtract_bitcast_fusion) | data formatting | bytes 37748736
  (142 shorter events, 55.9 us)
Async XLA Ops:
  7.2 92.4 %all-reduce.12.cloned.1.call-start = ((), (), s32[]{:S(2)}) async-start(), calls=%async_computation.1 | async-start | bytes 6291456 | tf_op jit(solution)/shard_map/psum | solution.py:11
  27.4 116.6 %all-reduce.14.cloned.1.call-start = ((), (), s32[]{:S(2)}) async-start(), calls=%async_computation.2 | async-start | bytes 524288 | tf_op jit(solution)/shard_map/psum | solution.py:43
  108.2 204.1 %all-reduce.22.cloned.1.call-start = ((), (), s32[]{:S(2)}) async-start(), calls=%async_computation.8 | async-start | bytes 3670016 | tf_op jit(solution)/shard_map/psum | solution.py:11
  234.8 309.2 %all-reduce.20.cloned.1.call-start = ((), (), s32[]{:S(2)}) async-start(), calls=%async_computation.7 | async-start | bytes 6291456 | tf_op jit(solution)/shard_map/psum | solution.py:49
  317.4 0.7 copy-start.6
  366.1 0.6 copy-start.7
  387.6 4.8 copy-start.4
  391.7 0.7 copy-start.3
  415.9 6.5 copy-start
  423.7 179.7 %all-reduce.16.cloned.1.call-start = ((), (), s32[]{:S(2)}) async-start(), calls=%async_computation.3 | async-start | bytes 524288 | tf_op jit(solution)/shard_map/psum | solution.py:53
  543.9 4.2 copy-start.1
  550.3 172.3 %all-reduce.18.cloned.1.call-start = ((), (), s32[]{:S(2)}) async-start(), calls=%async_computation.5 | async-start | bytes 524288 | tf_op jit(solution)/shard_map/psum | solution.py:11
  573.8 92.9 %copy-start.2 = (f32[256,1536]{1,0:T(8,128)S(1)}, f32[256,1536]{1,0:T(8,128)}, u32[]{:S(2)}) copy-start(f32[256,1536]{1,0:T(8,128)} %get-tuple-element.69) | copy-start | bytes 4718596
  669.1 118.6 %reduce-scatter.2.cloned.1.call-start = ((), (), s32[]{:S(2)}) async-start(), calls=%async_computation.4 | async-start | bytes 7077888 | tf_op jit(solution)/shard_map/reduce_scatter | solution.py:61
  713.3 124.0 %all-gather.2.cloned.1.call-start = ((), (), s32[]{:S(2)}) async-start(), calls=%async_computation.6 | async-start | bytes 7077888 | tf_op jit(solution)/shard_map/all_gather | solution.py:70
  722.6 63.2 %copy-start.5 = (f32[256,256]{1,0:T(8,128)S(1)}, f32[256,256]{1,0:T(8,128)}, u32[]{:S(2)}) copy-start(f32[256,256]{1,0:T(8,128)} %all-reduce.18.cloned.1.call-done) | copy-start | bytes 786436
  837.3 57.7 %slice-start = ((s8[18874368]{0:T(1024)(128)(4,1)}), s8[4194304]{0:T(1024)(128)(4,1)S(1)}, s32[]{:S(2)}) async-start(s8[18874368]{0:T(1024)(128)(4,1)} %bitcast.158), calls=%async_computation.9 | async-start | bytes 8388608
  837.3 57.7 %slice-start.1 = ((s8[18874368]{0:T(1024)(128)(4,1)}), s8[4194304]{0:T(1024)(128)(4,1)S(1)}, s32[]{:S(2)}) async-start(s8[18874368]{0:T(1024)(128)(4,1)} %bitcast.158), calls=%async_computation.10 | async-start | bytes 8388608
  837.3 57.7 %slice-start.2 = ((s8[18874368]{0:T(1024)(128)(4,1)}), s8[4194304]{0:T(1024)(128)(4,1)S(1)}, s32[]{:S(2)}) async-start(s8[18874368]{0:T(1024)(128)(4,1)} %bitcast.158), calls=%async_computation.11 | async-start | bytes 8388608
  872.5 22.5 %slice-start.3 = ((s8[18874368]{0:T(1024)(128)(4,1)}), s8[4194304]{0:T(1024)(128)(4,1)S(1)}, s32[]{:S(2)}) async-start(s8[18874368]{0:T(1024)(128)(4,1)} %bitcast.158), calls=%async_computation.12 | async-start | bytes 8388608
  872.5 22.5 %slice-start.4 = ((s8[18874368]{0:T(1024)(128)(4,1)}), s8[2097152]{0:T(1024)(128)(4,1)S(1)}, s32[]{:S(2)}) async-start(s8[18874368]{0:T(1024)(128)(4,1)} %bitcast.158), calls=%async_computation.13 | async-start | bytes 4194304
Sparse Core Ops, SparseCore 0:
  27.5 72.0 all-reduce.11
  108.4 35.6 all-reduce.13
  234.9 77.4 all-reduce.21
  423.8 120.0 all-reduce.19
  550.4 52.8 all-reduce.15
  669.2 53.3 all-reduce.17
  726.5 61.1 reduce-scatter.1
  792.0 45.2 all-gather.1
where the time goes:
time: 951 us; the launch traced here: 945 us
  waiting for transfers between devices  368 us (39%)
  other arithmetic  234 us (25%)
  matrix products  229 us (24%)
  local copies, waits for them, and re-layouts  92 us (10%)
  between operations  20 us (2%)
    dot_general x22, matrix products, matmul(): jnp.dot(left, right, precision=lax.Precision.HIGHEST, preferred_element_t...  220 us
    psum x3, waiting for transfers between devices, broadcast(): return lax.psum(jnp.where(mine, array, jnp.zeros_like(array)), axis)  136 us
    psum x1, waiting for transfers between devices, on_device(): lax.psum((matmul(vectors.T, amat), matmul(vectors.T, bmat)), 'row')  120 us
    another operation x14, other arithmetic, general_inverse(): lower = jnp.linalg.cholesky(matmul(square, square.T))  70.4 us
    unnamed x30, local copies, waits for them, and re-layouts  69.9 us
    another operation x13, other arithmetic, inverse_factor(): lower = jnp.linalg.cholesky(gram)  68.6 us
    all_gather x1, waiting for transfers between devices, on_device(): gathered = lax.all_gather(scaled, 'col', axis=0, tiled=True)  45.4 us
    another operation x4, other arithmetic, general_inverse(): linv = jax.scipy.linalg.solve_triangular(lower, ident, lower=True)  42.3 us
  transfers between devices with their start and end apart: 8, of which 8 were waited for; matrix products, arithmetic and copies ran while one was open for 16% of the time, Pallas kernels for 0%

commit v1 on v0

v1 whole, which is shorter than its diff:
```python
import jax
import jax.numpy as jnp
from jax import lax
from jax.sharding import PartitionSpec as P

NB = 256


def broadcast(array, axis, root):
    mine = lax.axis_index(axis) == root
    return lax.psum(jnp.where(mine, array, jnp.zeros_like(array)), axis)


def matmul(left, right):
    return jnp.dot(left, right, precision=lax.Precision.HIGHEST, preferred_element_type=jnp.float32)


def inverse_factor(gram):
    lower = jnp.linalg.cholesky(gram)
    ident = jnp.eye(gram.shape[0], dtype=jnp.float32)
    return jax.scipy.linalg.solve_triangular(lower, ident, lower=True).T


def general_inverse(square):
    lower = jnp.linalg.cholesky(matmul(square, square.T))
    ident = jnp.eye(square.shape[0], dtype=jnp.float32)
    linv = jax.scipy.linalg.solve_triangular(lower, ident, lower=True)
    return matmul(square.T, matmul(linv.T, linv))


def fast_matmul(left, right):
    return jnp.dot(left, right, precision=lax.Precision.HIGH, preferred_element_type=jnp.float32)


def on_device(pencil_a, pencil_b):
    rows_loc = pencil_a.shape[1]
    cols_loc = pencil_a.shape[3]
    amat = pencil_a.reshape(rows_loc, cols_loc)
    bmat = pencil_b.reshape(rows_loc, cols_loc)
    width = NB
    ident = jnp.eye(width, dtype=jnp.float32)
    row = lax.axis_index("row")
    col = lax.axis_index("col")
    last_row = lax.axis_size("row") - 1
    last_col = lax.axis_size("col") - 1
    top_mask = (row == 0).astype(jnp.float32)
    end_mask = (col == last_col).astype(jnp.float32)
    own_panel = amat[:, :width]
    own_strip = bmat[rows_loc - width :]
    zero = jnp.zeros((width, width), jnp.float32)
    small = jnp.stack(
        [
            jnp.where(col == 0, matmul(own_panel.T, own_panel), zero),
            jnp.where((col == 0) & (row == 0), own_panel[:width], zero),
            jnp.where(row == last_row, matmul(own_strip, own_strip.T), zero),
            jnp.where((col == last_col) & (row == last_row), own_strip[:, cols_loc - width :], zero),
        ]
    )
    small = lax.psum(small, ("row", "col"))
    own_panel, own_strip, small = lax.optimization_barrier((own_panel, own_strip, small))
    panel = broadcast(own_panel, "col", 0)
    strip = broadcast(own_strip, "row", last_row)
    left_inv = inverse_factor(small[0])
    right_inv = inverse_factor(small[2])
    vectors = matmul(panel, left_inv) + top_mask * jnp.pad(ident, ((0, rows_loc - width), (0, 0)))
    vectors_t = matmul(right_inv.T, strip) + end_mask * jnp.pad(
        ident, ((0, 0), (cols_loc - width, 0))
    )
    vectors, strip = lax.optimization_barrier((vectors, strip))
    products_a, products_b = lax.psum(
        (fast_matmul(vectors.T, amat), fast_matmul(vectors.T, bmat)), "row"
    )
    share = lax.psum_scatter(
        jnp.concatenate([fast_matmul(amat, vectors_t.T), fast_matmul(bmat, vectors_t.T)], axis=1),
        "col",
        scatter_dimension=0,
        tiled=True,
    )
    kinv_right = general_inverse(ident + matmul(right_inv.T, small[3]).T)
    kinv_left = general_inverse(ident + matmul(small[1], left_inv))
    scaled = jnp.concatenate(
        [matmul(share[:, :width], kinv_right.T), matmul(share[:, width:], kinv_right.T)], axis=1
    )
    gathered = lax.all_gather(scaled, "col", axis=0, tiled=True)
    cross = lax.psum(
        jnp.concatenate([matmul(products_a, vectors_t.T), matmul(products_b, vectors_t.T)], axis=0),
        "col",
    )

    def update(matrix, products, mixed, crossed):
        inner = products - matmul(matmul(crossed, kinv_right.T), vectors_t)
        low = jnp.concatenate([matmul(kinv_left, inner), vectors_t], axis=0)
        return matrix - fast_matmul(jnp.concatenate([vectors, mixed], axis=1), low)

    amat = update(amat, products_a, gathered[:, :width], cross[:width])
    bmat = update(bmat, products_b, gathered[:, width:], cross[width:])
    return (amat.reshape(1, rows_loc, 1, cols_loc), bmat.reshape(1, rows_loc, 1, cols_loc))


def solution(mesh):
    placed = (P("row", None, "col", None), P("row", None, "col", None))
    return jax.shard_map(
        on_device,
        mesh=mesh,
        in_specs=placed,
        out_specs=(P("row", None, "col", None), P("row", None, "col", None)),
        check_vma=False,
    )
```

time: 951 us -> 807 us (0.85)
  waiting for transfers between devices: 368 us -> 233 us
  matrix products: 229 us -> 167 us
  local copies, waits for them, and re-layouts: 92 us -> 140 us
    dot_general x22, matrix products: 220 us -> 42.6 us  [matmul(): jnp.dot(left, right, precision=lax.Precision.HIGHEST, preferred_element_t...]
    psum x3 -> x2, waiting for transfers between devices: 136 us -> 14.5 us  [broadcast(): return lax.psum(jnp.where(mine, array, jnp.zeros_like(array)), axis)]
    dot_general x0 -> x6, matrix products: none -> 109 us  [fast_matmul(): jnp.dot(left, right, precision=lax.Precision.HIGH, preferred_element_type...]
    reduce_scatter x1, waiting for transfers between devices: 1.33 us -> 58.9 us  [on_device(): lax.psum_scatter(jnp.concatenate([fast_matmul(amat, vectors_t.T), fast_ma...]
    psum x3, waiting for transfers between devices: 185 us -> 135 us  [the longest x1 130 us: on_device(): small = lax.psum(small, ('row', 'col'))]
    unnamed x30 -> x40, local copies, waits for them, and re-layouts: 69.9 us -> 108 us
    all_gather x1, waiting for transfers between devices: 45.4 us -> 24.6 us  [on_device(): gathered = lax.all_gather(scaled, 'col', axis=0, tiled=True)]
    slice x1 -> x4, local copies, waits for them, and re-layouts: 0.02 us -> 10.3 us  [the longest x1 5.06 us: on_device(): bmat = update(bmat, products_b, gathered[:, width:], cross[width:])]
  transfers between devices with their start and end apart: 8 -> 7, of which waited for: 8 -> 5; matrix products, arithmetic and copies ran while one was open for 16% -> 42% of each run, Pallas kernels for 0% -> 0%
where the time goes in v1:
time: 807 us; the launch traced here: 798 us
  other arithmetic  237 us (29%)
  waiting for transfers between devices  233 us (29%)
  matrix products  167 us (21%)
  local copies, waits for them, and re-layouts  140 us (17%)
  between operations  19.9 us (2%)
    psum x1, waiting for transfers between devices, on_device(): small = lax.psum(small, ('row', 'col'))  130 us
    dot_general x6, matrix products, fast_matmul(): jnp.dot(left, right, precision=lax.Precision.HIGH, preferred_element_type...  109 us
    unnamed x40, local copies, waits for them, and re-layouts  108 us
    another operation x14, other arithmetic, general_inverse(): lower = jnp.linalg.cholesky(matmul(square, square.T))  72.6 us
    another operation x14, other arithmetic, inverse_factor(): lower = jnp.linalg.cholesky(gram)  69.4 us
    reduce_scatter x1, waiting for transfers between devices, on_device(): lax.psum_scatter(jnp.concatenate([fast_matmul(amat, vectors_t.T), fast_ma...  58.9 us
    dot_general x22, matrix products, matmul(): jnp.dot(left, right, precision=lax.Precision.HIGHEST, preferred_element_t...  42.6 us
    another operation x4, other arithmetic, general_inverse(): linv = jax.scipy.linalg.solve_triangular(lower, ident, lower=True)  41.8 us
  transfers between devices with their start and end apart: 7, of which 5 were waited for; matrix products, arithmetic and copies ran while one was open for 42% of the time, Pallas kernels for 0%

profile of v1, /device:TPU:0, one launch (start us, length us, event | category | flops | bytes accessed | tf_op | source)
XLA Modules:
  0.0 798.0 jit_solution(4191456055535194326)
XLA Ops:
  10.0 2.6 fusion.14
  12.6 39.6 %copy.4 = f32[1,3072,1,1536]{1,3,2,0:T(8,128)} copy(f32[1,3072,1,1536]{3,2,1,0:T(1,128)} %param.5) | data formatting | bytes 37748736 | tf_op args[0]
  52.3 5.5 fusion.15
  60.0 3.9 slice.111
  63.9 129.5 %all-reduce.10.cloned.1.call-done = f32[4,256,256]{1,2,0:T(8,128)} async-done(((f32[4,256,256]{1,2,0:T(8,128)}), f32[4,256,256]{1,2,0:T(8,128)}) %all-reduce.10.cloned.1.call-update) | async-done | bytes 1048592 | tf_op jit(solution)/shard_map/psum | solution.py:59
  193.4 3.9 broadcast_select_fusion
  201.9 11.7 %cholesky.248 = f32[128,128]{1,0:T(8,128)S(1)} custom-call(f32[128,128]{1,0:T(8,128)S(1)} %cholesky.349), custom_call_target="Cholesky" | custom-call | tf_op jit(solution)/shard_map/jit(cholesky)/cholesky | solution.py:19
  214.5 11.7 %cholesky.214 = f32[128,128]{1,0:T(8,128)S(1)} custom-call(f32[128,128]{1,0:T(8,128)S(1)} %cholesky.346), custom_call_target="Cholesky" | custom-call | tf_op jit(solution)/shard_map/jit(cholesky)/cholesky | solution.py:19
  226.9 9.8 %custom-call.17 = f32[1,128,128]{1,2,0:T(8,128)S(1)} custom-call(f32[1,128,128]{2,1,0:T(8,128)S(1)} %get-tuple-element.107), custom_call_target="InvertDiagBlocksLowerTriangular" | custom-call | tf_op jit(solution)/shard_map/jit(cholesky)/cholesky | solution.py:19
  237.4 10.0 %custom-call.19 = f32[1,128,128]{1,2,0:T(8,128)S(1)} custom-call(f32[1,128,128]{2,1,0:T(8,128)S(1)} %get-tuple-element.103), custom_call_target="InvertDiagBlocksLowerTriangular" | custom-call | tf_op jit(solution)/shard_map/jit(cholesky)/cholesky | solution.py:19
  249.6 11.7 %cholesky.265 = f32[128,128]{1,0:T(8,128)S(1)} custom-call(f32[128,128]{1,0:T(8,128)S(1)} %convolution_subtract_fusion.8), custom_call_target="Cholesky" | custom-call | tf_op jit(solution)/shard_map/jit(cholesky)/cholesky | solution.py:19
  264.2 11.7 %cholesky.231 = f32[128,128]{1,0:T(8,128)S(1)} custom-call(f32[128,128]{1,0:T(8,128)S(1)} %convolution_subtract_fusion.9), custom_call_target="Cholesky" | custom-call | tf_op jit(solution)/shard_map/jit(cholesky)/cholesky | solution.py:19
  280.5 4.0 while.9
  284.9 3.9 while.8
  288.8 19.7 %custom-call.20 = f32[2,128,128]{1,2,0:T(8,128)S(1)} custom-call(f32[2,128,128]{2,1,0:T(8,128)S(1)} %get-tuple-element.39), custom_call_target="InvertDiagBlocksLowerTriangular" | custom-call | tf_op jit(solution)/shard_map/jit(_solve_triangular)/triangular_solve | solution.py:21
  308.5 19.7 %custom-call.18 = f32[2,128,128]{1,2,0:T(8,128)S(1)} custom-call(f32[2,128,128]{2,1,0:T(8,128)S(1)} %get-tuple-element.38), custom_call_target="InvertDiagBlocksLowerTriangular" | custom-call | tf_op jit(solution)/shard_map/jit(_solve_triangular)/triangular_solve | solution.py:21
  330.7 7.0 convolution_add_fusion
  337.7 14.5 %all-reduce.14.cloned.1.call-done = f32[256,1536]{0,1:T(8,128)} async-done(((f32[256,1536]{0,1:T(8,128)}), f32[256,1536]{0,1:T(8,128)}) %all-reduce.14.cloned.1.call-update) | async-done | bytes 1572880 | tf_op jit(solution)/shard_map/psum | solution.py:11
  352.2 17.5 %fusion = f32[256,1536]{1,0:T(8,128)} fusion(f32[3072,256]{1,0:T(8,128)S(1)} %convolution_add_fusion, f32[1,3072,1,1536]{3,2,1,0:T(1,128)} %param.6), kind=kOutput, calls=%fused_computation.9 | convolution fusion | flops 7247757312 | bytes 23592960 | tf_op jit(solution)/shard_map/dot_general | solution.py:32
  369.6 19.3 %fusion.80 = f32[256,1536]{1,0:T(8,128)} fusion(f32[3072,256]{1,0:T(8,128)S(1)} %convolution_add_fusion, f32[1,3072,1,1536]{1,3,2,0:T(8,128)} %copy.4), kind=kOutput, calls=%fused_computation.170 | convolution fusion | flops 7247757312 | bytes 23592960 | tf_op jit(solution)/shard_map/dot_general | solution.py:32
  391.2 2.9 convolution_add_fusion.1
  394.2 15.4 %fusion.9 = f32[3072,256]{0,1:T(8,128)S(1)} fusion(f32[256,1536]{1,0:T(8,128)S(1)} %convolution_add_fusion.1, f32[1,3072,1,1536]{3,2,1,0:T(1,128)} %param.6), kind=kOutput, calls=%fused_computation.22 | convolution fusion | flops 7247757312 | bytes 23592960 | tf_op jit(solution)/shard_map/dot_general | solution.py:32
  409.6 11.9 %convolution_bitcast_fusion = f32[3072,256]{0,1:T(8,128)S(1)} fusion(f32[256,1536]{1,0:T(8,128)S(1)} %convolution_add_fusion.1, f32[1,3072,1,1536]{1,3,2,0:T(8,128)} %copy.4), kind=kOutput, calls=%fused_computation.23 | convolution fusion | flops 7247757312 | bytes 23592960 | tf_op jit(solution)/shard_map/dot_general | solution.py:32
  421.5 3.1 pad_maximum_fusion.4
  429.2 11.7 %cholesky.282 = f32[128,128]{1,0:T(8,128)S(1)} custom-call(f32[128,128]{1,0:T(8,128)S(1)} %cholesky.352), custom_call_target="Cholesky" | custom-call | tf_op jit(solution)/shard_map/jit(cholesky)/cholesky | solution.py:25
  441.5 10.4 %custom-call.21 = f32[1,128,128]{1,2,0:T(8,128)} custom-call(f32[1,128,128]{2,1,0:T(8,128)S(1)} %get-tuple-element.99), custom_call_target="InvertDiagBlocksLowerTriangular" | custom-call | tf_op jit(solution)/shard_map/jit(cholesky)/cholesky | solution.py:25
  455.6 13.2 %cholesky.299 = f32[128,128]{1,0:T(8,128)} custom-call(f32[128,128]{1,0:T(8,128)} %convolution_subtract_fusion.7), custom_call_target="Cholesky" | custom-call | tf_op jit(solution)/shard_map/jit(cholesky)/cholesky | solution.py:25
  474.0 5.3 while.10
  474.8 2.0 bitcast_dynamic-update-slice_fusion.10
  477.3 2.0 bitcast_dynamic-update-slice_fusion.10
  479.3 21.1 %custom-call.22 = f32[2,128,128]{1,2,0:T(8,128)} custom-call(f32[2,128,128]{2,1,0:T(8,128)} %get-tuple-element.40), custom_call_target="InvertDiagBlocksLowerTriangular" | custom-call | tf_op jit(solution)/shard_map/jit(_solve_triangular)/triangular_solve | solution.py:27
  504.2 5.0 all-reduce.18.cloned.1.call-done
  509.1 3.0 fusion.93
  514.7 58.9 %reduce-scatter.2.cloned.1.call-done = f32[384,512]{0,1:T(8,128)} async-done(((f32[3072,512]{0,1:T(8,128)}), f32[384,512]{0,1:T(8,128)}) %reduce-scatter.2.cloned.1.call-update) | async-done | bytes 786448 | tf_op jit(solution)/shard_map/reduce_scatter | solution.py:73
  575.4 1.8 fusion.18
  580.4 11.7 %cholesky.316 = f32[128,128]{1,0:T(8,128)S(1)} custom-call(f32[128,128]{1,0:T(8,128)S(1)} %cholesky.355), custom_call_target="Cholesky" | custom-call | tf_op jit(solution)/shard_map/jit(cholesky)/cholesky | solution.py:25
  592.1 9.8 %custom-call.23 = f32[1,128,128]{1,2,0:T(8,128)S(1)} custom-call(f32[1,128,128]{2,1,0:T(8,128)S(1)} %get-tuple-element.95), custom_call_target="InvertDiagBlocksLowerTriangular" | custom-call | tf_op jit(solution)/shard_map/jit(cholesky)/cholesky | solution.py:25
  602.4 12.1 %cholesky.333 = f32[128,128]{1,0:T(8,128)S(1)} custom-call(f32[128,128]{1,0:T(8,128)S(1)} %convolution_subtract_fusion.6), custom_call_target="Cholesky" | custom-call | tf_op jit(solution)/shard_map/jit(cholesky)/cholesky | solution.py:25
  617.1 3.8 while.11
  620.9 19.7 %custom-call.24 = f32[2,128,128]{1,2,0:T(8,128)S(1)} custom-call(f32[2,128,128]{2,1,0:T(8,128)S(1)} %get-tuple-element.41), custom_call_target="InvertDiagBlocksLowerTriangular" | custom-call | tf_op jit(solution)/shard_map/jit(_solve_triangular)/triangular_solve | solution.py:27
  642.1 2.2 fusion.92
  651.6 2.6 fusion.95
  654.2 24.6 %all-gather.2.cloned.1.call-done = f32[3072,512]{1,0:T(8,128)} async-done(((f32[384,512]{1,0:T(8,128)}), f32[3072,512]{1,0:T(8,128)}) %all-gather.2.cloned.1.call-update) | async-done | bytes 6291472 | tf_op jit(solution)/shard_map/all_gather | solution.py:84
  678.8 5.1 fusion.88
  683.9 20.7 %subtract_bitcast_fusion = f32[1,3072,1,1536]{1,3,2,0:T(8,128)} fusion(f32[3072,256]{1,0:T(8,128)S(1)} %copy-done.1, f32[3072,256]{1,0:T(8,128)S(1)} %get-tuple-element.87, f32[256,1536]{1,0:T(8,128)S(1)} %convolution_add_fusion.1, f32[256,1536]{1,0:T(8,128)S(1)} %copy-done.2, f32[1,3072,1,1536]{1,3,2,0:T(8,128)} %copy.4), kind=kOutput, calls=%fused_computation.14 | convolution fusion | flops 14502592512 | bytes 47185920 | tf_op jit(solution)/shard_map/dot_general | solution.py:32
  704.5 39.7 %copy.15 = f32[1,3072,1,1536]{3,2,1,0:T(1,128)} copy(f32[1,3072,1,1536]{1,3,2,0:T(8,128)} %subtract_bitcast_fusion) | data formatting | bytes 37748736
  744.2 24.4 %fusion.4 = f32[1,3072,1,1536]{3,1,2,0:T(8,128)} fusion(f32[1,3072,1,1536]{3,2,1,0:T(1,128)} %param.6, f32[3072,256]{1,0:T(8,128)} %copy-done, f32[3072,256]{1,0:T(8,128)} %get-tuple-element.86, f32[256,1536]{1,0:T(8,128)S(1)} %convolution_add_fusion.1, f32[256,1536]{1,0:T(8,128)S(1)} %fusion.96), kind=kOutput, calls=%fused_computation.13 | convolution fusion | flops 14502592512 | bytes 47185920 | tf_op jit(solution)/shard_map/dot_general | solution.py:32
  768.6 22.3 %copy.16 = f32[1,3072,1,1536]{3,2,1,0:T(1,128)} copy(f32[1,3072,1,1536]{3,1,2,0:T(8,128)} %fusion.4) | data formatting | bytes 37748736
  (159 shorter events, 71.4 us)
Async XLA Ops:
  7.2 1.4 slice-start
  7.2 186.2 %all-reduce.10.cloned.1.call-start = ((), (), s32[]{:S(2)}) async-start(), calls=%async_computation.1 | async-start | bytes 2097152 | tf_op jit(solution)/shard_map/psum | solution.py:59
  59.9 270.8 %all-reduce.12.cloned.1.call-start = ((), (), s32[]{:S(2)}) async-start(), calls=%async_computation.2 | async-start | bytes 6291456 | tf_op jit(solution)/shard_map/psum | solution.py:11
  197.3 1.2 copy-start.7
  197.3 154.9 %all-reduce.14.cloned.1.call-start = ((), (), s32[]{:S(2)}) async-start(), calls=%async_computation.3 | async-start | bytes 3145728 | tf_op jit(solution)/shard_map/psum | solution.py:11
  201.2 0.7 copy-start.14
  284.4 46.3 %copy-start.11 = (f32[256,256]{1,0:T(8,128)}, f32[256,256]{1,0:T(8,128)S(1)}, u32[]{:S(2)}) copy-start(f32[256,256]{1,0:T(8,128)S(1)} %get-tuple-element.325) | copy-start | bytes 786436
  284.5 224.7 %all-reduce.18.cloned.1.call-start = ((), (), s32[]{:S(2)}) async-start(), calls=%async_computation.7 | async-start | bytes 6291456 | tf_op jit(solution)/shard_map/psum | solution.py:70
  308.5 20.7 %copy-start.16 = (f32[2,128,128]{1,2,0:T(8,128)}, f32[2,128,128]{1,2,0:T(8,128)S(1)}, u32[]{:S(2)}) copy-start(f32[2,128,128]{1,2,0:T(8,128)S(1)} %custom-call.20) | copy-start | bytes 393220
  337.7 32.0 %copy-start = (f32[3072,256]{1,0:T(8,128)}, f32[3072,256]{1,0:T(8,128)S(1)}, u32[]{:S(2)}) copy-start(f32[3072,256]{1,0:T(8,128)S(1)} %convolution_add_fusion) | copy-start | bytes 9437188
  388.9 0.9 copy-start.10
  388.9 2.0 copy-start.17
  388.9 184.7 %reduce-scatter.2.cloned.1.call-start = ((), (), s32[]{:S(2)}) async-start(), calls=%async_computation.4 | async-start | bytes 7077888 | tf_op jit(solution)/shard_map/reduce_scatter | solution.py:73
  424.6 1.2 copy-start.8
  424.6 219.8 %all-reduce.16.cloned.1.call-start = ((), (), s32[]{:S(2)}) async-start(), calls=%async_computation.6 | async-start | bytes 1048576 | tf_op jit(solution)/shard_map/psum | solution.py:85
  428.5 0.7 copy-start.13
  440.9 0.6 copy-start.15
  470.4 1.9 copy-start.12
  509.1 3.0 copy-start.4
  514.5 164.3 %all-gather.2.cloned.1.call-start = ((), (), s32[]{:S(2)}) async-start(), calls=%async_computation.5 | async-start | bytes 7077888 | tf_op jit(solution)/shard_map/all_gather | solution.py:84
  579.7 61.2 %copy-start.6 = (f32[256,256]{1,0:T(8,128)}, f32[256,256]{1,0:T(8,128)S(1)}, u32[]{:S(2)}) copy-start(f32[256,256]{1,0:T(8,128)S(1)} %convolution_add_fusion.2) | copy-start | bytes 786436
  641.2 6.0 copy-start.5
  644.4 4.3 copy-start.9
  647.2 3.0 copy-start.3
  678.8 5.1 copy-start.1
  678.8 5.1 copy-start.2
Sparse Core Ops, SparseCore 0:
  60.0 133.3 all-reduce.9
  197.4 68.5 all-reduce.11
  284.6 67.5 all-reduce.13
  389.1 120.0 all-reduce.17
  512.9 60.6 reduce-scatter.1
  576.6 55.6 all-reduce.15
  634.2 44.5 all-gather.1
